TPU v7x, 256 devices: a whole 4x4x8 slice. The times are simulated.
256 devices in a mesh: section: 32 (over z, y), dp: 4 (over x), mp: 2 (over core).
Axes of the slice: x: 4, y: 4, z: 8, core: 2. Of those that a mesh axis runs over, the one named last changes fastest.
Arguments:
- inputs: bfloat16 [4, 128, 8192], P(None, 'dp'), may hold values from -12.7 to 12.7
- value_weight: bfloat16 [32, 8192, 1024], P('section', None, 'mp'), may hold values from -0.13975425 to 0.13975425
- carry_gain: float32 [32, 8192], P('section'), may hold values from 0.6 to 1.4
- channel_bins: int32 [32, 8192], P('section'), may hold values from 0 to 15
- grid_picks: int32 [32, 20], P('section'), may hold values from 0 to 19, each once within a row
Outputs:
- quant_out: bfloat16 [32, 4, 128, 1024], P('section', None, 'dp', 'mp')
- grid_loss: float32 [32, 4], P('section')
Inputs may be any that keep to these rules, and one draw needn't show every extreme that they name: `grid_picks`: each row lists every grid point once.
All inputs are finite; a program needn't handle non-finite values.
Results may differ from a plain program's by a relative error of at most 0.029.
Values may be sent and summed in bfloat16 or wider, within the bound.
A program may use at most 192 MiB of HBM per device.

v0:
```python
import math
import jax
import jax.numpy as jnp
from jax import lax
from jax.sharding import PartitionSpec as P

D = 8192
KV = 1024
HEAD = 128
GROUP = 128
GRID = 20
PICKS = 4
EPS = 1e-06
LOSS_UNIT = 1000.0
TWO_PI = 2.0 * math.pi


def sent_to_all(value, axis):
    peers = lax.axis_size(axis)
    return lax.all_to_all(
        jnp.broadcast_to(value[None], (peers, *value.shape)), axis, 0, 0, tiled=True
    )


def over_copies(value, axis):
    everything = sent_to_all(value, axis)
    return jnp.sum(everything, axis=0)


def from_behind(block, axis, distance):
    devices = range(lax.axis_size(axis))
    route = [(i - distance, i) for i in devices if i - distance in devices]
    return lax.ppermute(block, axis, route)


def quantize(weight, channel_bin, grid_pick):
    exponent = grid_pick.astype(jnp.float32) / GRID
    scaling = jnp.exp2(exponent * channel_bin.astype(jnp.float32) / 4.0)
    scaled = weight.astype(jnp.float32) * scaling[:, None]
    blocks = scaled.reshape(scaled.shape[0] // GROUP, GROUP, scaled.shape[1])
    spacing = (jnp.max(jnp.abs(blocks), axis=1, keepdims=True) + EPS) / 7.0
    levels = blocks / spacing
    snapped = (levels - jnp.sin(TWO_PI * levels) / TWO_PI) * spacing
    return (snapped.reshape(scaled.shape) / scaling[:, None]).astype(jnp.bfloat16)


def repeat_heads(values):
    row_count, columns = values.shape
    head_view = values.reshape(row_count, columns // HEAD, 1, HEAD)
    spread = jnp.broadcast_to(head_view, (row_count, columns // HEAD, D // KV, HEAD))
    return spread.reshape(row_count, columns * (D // KV))


def local(inputs, value_weight, carry_gain, channel_bins, grid_picks):
    section_count = lax.axis_size("section")
    section_index = lax.axis_index("section")
    micro_count, row_count, model_width = inputs.shape
    weight = value_weight[0]
    gain_row = carry_gain[0]
    half_width = weight.shape[1]
    stacked = jnp.concatenate(
        [
            quantize(weight, channel_bins[0], grid_picks[0, pick_index])
            for pick_index in range(PICKS)
        ],
        axis=1,
    )
    residual_gain = 1.0 / math.sqrt(section_count)
    tick_count = section_count + micro_count - 1

    def grid_pass(stream):
        exact = jnp.dot(stream, weight, preferred_element_type=jnp.float32)
        candidate = jnp.dot(stream, stacked, preferred_element_type=jnp.float32).reshape(
            row_count, PICKS, half_width
        )
        errors = jnp.sum(jnp.square(candidate - exact[:, None, :]), axis=(0, 2))
        return (candidate[:, 0, :].astype(jnp.bfloat16), errors)

    def spare_pass(stream):
        return (jnp.zeros((row_count, half_width), jnp.bfloat16), jnp.zeros((PICKS,), jnp.float32))

    def advance(tick_index, state_tuple):
        received, outputs, totals = state_tuple
        slot_index = tick_index - section_index
        active = jnp.logical_and(slot_index >= 0, slot_index < micro_count)
        clamped = jnp.clip(slot_index, 0, micro_count - 1)
        entry_rows = lax.dynamic_index_in_dim(inputs, clamped, 0, keepdims=False)
        stream = jnp.where(section_index == 0, entry_rows, received)
        chosen, errors = lax.cond(active, grid_pass, spare_pass, stream)
        previous = lax.dynamic_index_in_dim(outputs, clamped, 0, keepdims=False)
        outputs = lax.dynamic_update_index_in_dim(
            outputs, jnp.where(active, chosen, previous), clamped, 0
        )
        totals = totals + over_copies(errors, ("dp", "mp"))
        part_width = model_width // lax.axis_size("mp")
        part_start = lax.axis_index("mp") * part_width
        own_features = lax.dynamic_slice_in_dim(stream, part_start, part_width, 1)
        own_gain = lax.dynamic_slice_in_dim(gain_row, part_start, part_width, 0)
        next_part = (
            own_features.astype(jnp.float32) * own_gain[None, :]
            + residual_gain * repeat_heads(chosen).astype(jnp.float32)
        ).astype(jnp.bfloat16)
        arrived = from_behind(next_part, "section", 1)
        received = lax.all_gather(arrived, "mp", axis=1, tiled=True)
        return (received, outputs, totals)

    initial = (
        jnp.zeros((row_count, model_width), jnp.bfloat16),
        jnp.zeros((micro_count, row_count, half_width), jnp.bfloat16),
        jnp.zeros((PICKS,), jnp.float32),
    )
    received, outputs, totals = lax.fori_loop(0, tick_count, advance, initial)
    entry_count = micro_count * row_count * lax.axis_size("dp") * half_width * lax.axis_size("mp")
    grid_loss = totals * LOSS_UNIT / entry_count
    return (outputs[None], grid_loss[None])


def solution(mesh):
    placed = (
        P(None, "dp", None),
        P("section", None, "mp"),
        P("section", None),
        P("section", None),
        P("section", None),
    )
    return jax.shard_map(
        local,
        mesh=mesh,
        in_specs=placed,
        out_specs=(P("section", None, "dp", "mp"), P("section", None)),
        check_vma=False,
    )
```

profile of v0, /device:TPU:241, one launch (start us, length us, event | category | flops | bytes accessed | tf_op | source)
XLA Modules:
  0.0 1432.9 jit_solution(17592622582749549896)
XLA Ops:
  5.6 12.4 fusion.11
  18.1 246.1 %fusion.3 = (bf16[8192,512]{1,0:T(8,128)(2,1)}, bf16[8192,512]{1,0:T(8,128)(2,1)}, bf16[8192,512]{1,0:T(8,128)(2,1)}, bf16[8192,512]{1,0:T(8,128)(2,1)}) fusion(f32[64,512]{1,0:T(8,128)S(1)} %get-tuple-element.292, f32[8192]{0:T(1024)S(1)} %bitcast.105, bf16[1,8192,512]{2,1,0:T(8,128)(2,1)} %param.10, f32[64,512]{1,0:T(8,128)S(1)} %get-tuple-element.289, ...), kind=kLoop, calls=%fused_computation.29 | loop fusion | flops 138412032 | bytes 42598400 | tf_op jit(solution)/shard_map/convert_element_type | solution.py:44
  264.2 22.7 %pad_maximum_fusion = bf16[8192,2048]{1,0:T(8,128)(2,1)} fusion(bf16[8192,512]{1,0:T(8,128)(2,1)} %get-tuple-element.278, bf16[8192,512]{1,0:T(8,128)(2,1)} %get-tuple-element.279, bf16[8192,512]{1,0:T(8,128)(2,1)} %get-tuple-element.280, bf16[8192,512]{1,0:T(8,128)(2,1)} %get-tuple-element.277), kind=kLoop, calls=%fused_computation.11 | loop fusion | flops 134217728 | bytes 67108864 | tf_op jit(solution)/shard_map/concatenate | solution.py:61
  287.0 1145.3 %while.19 = (s32[]{:T(128)}, bf16[32,8192]{1,0:T(8,128)(2,1)S(1)}, bf16[4,32,512]{2,1,0:T(8,128)(2,1)S(1)}, f32[4]{0:T(128)S(1)}, pred[]{:T(512)}, /*index=5*/s3...) while((s32[]{:T(128)}, bf16[32,8192]{1,0:T(8,128)(2,1)S(1)}, ...), condition=%wide.region_10.11_spmd.clone, body=%wide.region_4.10_spmd.clone.sunk | while | flops 1343275008 | bytes 50324384 | solution.py:112
  292.4 5.3 all-to-all-start
  312.4 4.5 all-to-all-done
  327.3 4.5 all-to-all-done
  342.1 4.5 all-to-all-done
  356.9 4.5 all-to-all-done
  371.7 4.5 all-to-all-done
  386.9 4.5 all-to-all-done
  403.0 4.5 all-to-all-done
  419.1 4.5 all-to-all-done
  435.3 4.5 all-to-all-done
  451.4 4.5 all-to-all-done
  467.5 4.5 all-to-all-done
  483.7 4.5 all-to-all-done
  499.8 4.5 all-to-all-done
  515.9 4.5 all-to-all-done
  532.1 4.5 all-to-all-done
  548.2 4.5 all-to-all-done
  564.3 4.5 all-to-all-done
  580.5 4.5 all-to-all-done
  596.6 4.5 all-to-all-done
  612.8 4.5 all-to-all-done
  628.9 4.5 all-to-all-done
  645.0 4.5 all-to-all-done
  725.7 4.5 all-to-all-done
  741.8 4.5 all-to-all-done
  762.5 490.0 %collective-permute-done = bf16[32,4096]{1,0:T(8,128)(2,1)S(1)} collective-permute-done((bf16[32,4096]{1,0:T(8,128)(2,1)S(1)}, bf16[32,4096]{1,0:T(8,128)(2,1)S(1)}, u32[]{:S(2)}, u32[]{:S(2)}) %collective-permute-start) | collective-permute-done | bytes 262176 | tf_op jit(solution)/shard_map/while/body/eval_jaxpr/ppermute | solution.py:33
  1256.4 19.0 %conditional.3 = (bf16[32,512]{1,0:T(8,128)(2,1)S(1)}, f32[4]{0:T(128)S(1)}, f32[32,512]{1,0:T(8,128)S(1)}) conditional(s32[]{:T(128)} %convert_element_type.178, () %tuple.72, (bf16[32,8192]{1,0:T(8,128)(2,1)S(1)}, bf16[8192,2048]{1,0:T(8,128)(2,1)}, bf16[8192,512]{1,0:T(8,128)(2,1)}) %tuple.73), branch_computations={%region_5.5_spmd, %region_6.8_spmd} | conditional | flops 1342455808 | bytes 44793900 | solution.py:89
  1256.4 4.9 fusion.20
  1261.5 13.6 multiply_reduce_fusion
  1278.3 4.9 all-to-all-start
  1292.6 19.0 %conditional.3 = (bf16[32,512]{1,0:T(8,128)(2,1)S(1)}, f32[4]{0:T(128)S(1)}, f32[32,512]{1,0:T(8,128)S(1)}) conditional(s32[]{:T(128)} %convert_element_type.178, () %tuple.72, (bf16[32,8192]{1,0:T(8,128)(2,1)S(1)}, bf16[8192,2048]{1,0:T(8,128)(2,1)}, bf16[8192,512]{1,0:T(8,128)(2,1)}) %tuple.73), branch_computations={%region_5.5_spmd, %region_6.8_spmd} | conditional | flops 1342455808 | bytes 44793900 | solution.py:89
  1292.7 4.9 fusion.20
  1297.7 13.6 multiply_reduce_fusion
  1314.6 4.9 all-to-all-start
  1328.9 19.0 %conditional.3 = (bf16[32,512]{1,0:T(8,128)(2,1)S(1)}, f32[4]{0:T(128)S(1)}, f32[32,512]{1,0:T(8,128)S(1)}) conditional(s32[]{:T(128)} %convert_element_type.178, () %tuple.72, (bf16[32,8192]{1,0:T(8,128)(2,1)S(1)}, bf16[8192,2048]{1,0:T(8,128)(2,1)}, bf16[8192,512]{1,0:T(8,128)(2,1)}) %tuple.73), branch_computations={%region_5.5_spmd, %region_6.8_spmd} | conditional | flops 1342455808 | bytes 44793900 | solution.py:89
  1328.9 4.9 fusion.20
  1334.0 13.6 multiply_reduce_fusion
  1350.8 4.9 all-to-all-start
  1365.1 19.0 %conditional.3 = (bf16[32,512]{1,0:T(8,128)(2,1)S(1)}, f32[4]{0:T(128)S(1)}, f32[32,512]{1,0:T(8,128)S(1)}) conditional(s32[]{:T(128)} %convert_element_type.178, () %tuple.72, (bf16[32,8192]{1,0:T(8,128)(2,1)S(1)}, bf16[8192,2048]{1,0:T(8,128)(2,1)}, bf16[8192,512]{1,0:T(8,128)(2,1)}) %tuple.73), branch_computations={%region_5.5_spmd, %region_6.8_spmd} | conditional | flops 1342455808 | bytes 44793900 | solution.py:89
  1365.2 4.9 fusion.20
  1370.2 13.6 multiply_reduce_fusion
  1387.1 4.9 all-to-all-start
  1400.7 18.7 %collective-permute-start = (bf16[32,4096]{1,0:T(8,128)(2,1)S(1)}, bf16[32,4096]{1,0:T(8,128)(2,1)S(1)}, u32[]{:S(2)}, u32[]{:S(2)}) collective-permute-start(bf16[32,4096]{1,0:T(8,128)(2,1)S(1)} %fusion.27), channel_id=1, source_target_pairs={{0,8},{8,16},{16,24},{24,32},{32,40},{40,48},{48,56},{56,64},{64,7... | collective-permute-start | bytes 786440 | tf_op jit(solution)/shard_map/while/body/eval_jaxpr/ppermute | solution.py:33
  1420.0 5.2 all-to-all-start
  (692 shorter events, 424.7 us)
Async XLA Ops:
  288.8 13.3 collective-permute-start
  292.4 9.8 all-to-all-start
  306.3 10.7 collective-permute-start
  321.1 10.7 collective-permute-start
  335.9 10.7 collective-permute-start
  350.8 10.7 collective-permute-start
  365.6 10.8 collective-permute-start
  368.1 8.1 all-to-all-start
  380.7 11.8 collective-permute-start
  396.9 11.8 collective-permute-start
  413.0 11.8 collective-permute-start
  429.1 11.8 collective-permute-start
  431.7 8.1 all-to-all-start
  445.3 11.8 collective-permute-start
  461.4 11.8 collective-permute-start
  477.5 11.8 collective-permute-start
  493.7 11.8 collective-permute-start
  509.8 11.8 collective-permute-start
  525.9 11.8 collective-permute-start
  528.5 8.1 all-to-all-start
  542.1 11.8 collective-permute-start
  544.6 8.1 all-to-all-start
  558.2 11.8 collective-permute-start
  574.3 11.8 collective-permute-start
  590.5 11.8 collective-permute-start
  606.6 11.8 collective-permute-start
  622.7 11.8 collective-permute-start
  625.3 8.1 all-to-all-start
  638.9 11.8 collective-permute-start
  641.4 8.1 all-to-all-start
  655.0 11.8 collective-permute-start
  671.2 11.8 collective-permute-start
  687.3 11.8 collective-permute-start
  703.4 11.8 collective-permute-start
  719.6 11.8 collective-permute-start
  735.7 11.8 collective-permute-start
  738.2 8.1 all-to-all-start
  751.8 500.7 %collective-permute-start = (bf16[32,4096]{1,0:T(8,128)(2,1)S(1)}, bf16[32,4096]{1,0:T(8,128)(2,1)S(1)}, u32[]{:S(2)}, u32[]{:S(2)}) collective-permute-start(bf16[32,4096]{1,0:T(8,128)(2,1)S(1)} %fusion.27), channel_id=1, source_target_pairs={{0,8},{8,16},{16,24},{24,32},{32,40},{40,48},{48,56},{56,64},{64,7... | collective-permute-start | bytes 786440 | tf_op jit(solution)/shard_map/while/body/eval_jaxpr/ppermute | solution.py:33
  1275.8 13.0 collective-permute-start
  1278.3 9.4 all-to-all-start
  1312.1 13.0 collective-permute-start
  1314.6 9.4 all-to-all-start
  1348.3 13.0 collective-permute-start
  1350.8 9.4 all-to-all-start
  1384.6 12.0 collective-permute-start
  1387.1 9.4 all-to-all-start
  1400.7 29.1 %collective-permute-start = (bf16[32,4096]{1,0:T(8,128)(2,1)S(1)}, bf16[32,4096]{1,0:T(8,128)(2,1)S(1)}, u32[]{:S(2)}, u32[]{:S(2)}) collective-permute-start(bf16[32,4096]{1,0:T(8,128)(2,1)S(1)} %fusion.27), channel_id=1, source_target_pairs={{0,8},{8,16},{16,24},{24,32},{32,40},{40,48},{48,56},{56,64},{64,7... | collective-permute-start | bytes 786440 | tf_op jit(solution)/shard_map/while/body/eval_jaxpr/ppermute | solution.py:33
  1420.0 9.7 all-to-all-start
  (24 other events, 202.3 us)
where the time goes:
time: 1440 us; the launch traced here: 1430 us
  waiting for transfers between devices  676 us (47%)
  other arithmetic  335 us (23%)
  starting transfers between devices  219 us (15%)
  blocking collectives  94.4 us (7%)
  matrix products  74 us (5%)
  local copies, waits for them, and re-layouts  27.1 us (2%)
    ppermute x35, waiting for transfers between devices, from_behind(): return lax.ppermute(block, axis, route)  518 us
    convert_element_type x1, other arithmetic, quantize(): (snapped.reshape(scaled.shape) / scaling[:, None]).astype(jnp.bfloat16)  246 us
    all_to_all x35, waiting for transfers between devices, sent_to_all(): lax.all_to_all(jnp.broadcast_to(value[None], (peers, *value.shape)), axis...  158 us
    all_to_all x35, starting transfers between devices, sent_to_all(): lax.all_to_all(jnp.broadcast_to(value[None], (peers, *value.shape)), axis...  134 us
    all_gather x35, blocking collectives, advance(): received = lax.all_gather(arrived, 'mp', axis=1, tiled=True)  94.4 us
    ppermute x35, starting transfers between devices, from_behind(): return lax.ppermute(block, axis, route)  85 us
    dot_general x4, matrix products, grid_pass(): jnp.dot(stream, stacked, preferred_element_type=jnp.float32)  54.4 us
    select_n x35, other arithmetic, advance(): stream = jnp.where(section_index == 0, entry_rows, received)  38.4 us
  transfers between devices with their start and end apart: 70, of which 63 were waited for; matrix products, arithmetic and copies ran while one was open for 2% of the time, Pallas kernels for 0%

commit v1 on v0

--- a/solution.py
+++ b/solution.py
@@ -101,7 +101,9 @@
             + residual_gain * repeat_heads(chosen).astype(jnp.float32)
         ).astype(jnp.bfloat16)
         arrived = from_behind(next_part, "section", 1)
-        received = lax.all_gather(arrived, "mp", axis=1, tiled=True)
+        received = jnp.concatenate(
+            lax.all_to_all(jnp.stack([arrived] * lax.axis_size("mp")), "mp", 0, 0), axis=1
+        )
         return (received, outputs, totals)
 
     initial = (

time: 1440 us -> 1510 us (1.049)
  blocking collectives: 94.4 us -> 164 us
    all_to_all x0 -> x35, blocking collectives: none -> 164 us  [advance(): lax.all_to_all(jnp.stack([arrived] * lax.axis_size('mp')), 'mp', 0, 0)]
    all_gather x35 -> x0, blocking collectives: 94.4 us -> none  [advance(): received = lax.all_gather(arrived, 'mp', axis=1, tiled=True)]
where the time goes in v1:
time: 1510 us
  waiting for transfers between devices  676 us (45%)
  other arithmetic  337 us (22%)
  starting transfers between devices  219 us (15%)
  blocking collectives  164 us (11%)
  matrix products  74 us (5%)
  local copies, waits for them, and re-layouts  28.3 us (2%)
    ppermute x35, waiting for transfers between devices, from_behind(): return lax.ppermute(block, axis, route)  518 us
    convert_element_type x1, other arithmetic, quantize(): (snapped.reshape(scaled.shape) / scaling[:, None]).astype(jnp.bfloat16)  246 us
    all_to_all x35, blocking collectives, advance(): lax.all_to_all(jnp.stack([arrived] * lax.axis_size('mp')), 'mp', 0, 0)  164 us
    all_to_all x35, waiting for transfers between devices, sent_to_all(): lax.all_to_all(jnp.broadcast_to(value[None], (peers, *value.shape)), axis...  158 us
    all_to_all x35, starting transfers between devices, sent_to_all(): lax.all_to_all(jnp.broadcast_to(value[None], (peers, *value.shape)), axis...  134 us
    ppermute x35, starting transfers between devices, from_behind(): return lax.ppermute(block, axis, route)  85 us
    dot_general x4, matrix products, grid_pass(): jnp.dot(stream, stacked, preferred_element_type=jnp.float32)  54.4 us
    select_n x35, other arithmetic, advance(): stream = jnp.where(section_index == 0, entry_rows, received)  38.7 us
  transfers between devices with their start and end apart: 70, of which 63 were waited for; matrix products, arithmetic and copies ran while one was open for 2% of the time, Pallas kernels for 0%

profile of v1, /device:TPU:241, one launch (start us, length us, event | category | flops | bytes accessed | tf_op | source)
XLA Modules:
  0.0 1506.5 jit_solution(8149324114972896499)
XLA Ops:
  5.6 12.4 fusion.11
  18.1 246.1 %fusion.3 = (bf16[8192,512]{1,0:T(8,128)(2,1)}, bf16[8192,512]{1,0:T(8,128)(2,1)}, bf16[8192,512]{1,0:T(8,128)(2,1)}, bf16[8192,512]{1,0:T(8,128)(2,1)}) fusion(f32[64,512]{1,0:T(8,128)S(1)} %get-tuple-element.292, f32[8192]{0:T(1024)S(1)} %bitcast.118, bf16[1,8192,512]{2,1,0:T(8,128)(2,1)} %param.10, f32[64,512]{1,0:T(8,128)S(1)} %get-tuple-element.289, ...), kind=kLoop, calls=%fused_computation.30 | loop fusion | flops 138412032 | bytes 42598400 | tf_op jit(solution)/shard_map/convert_element_type | solution.py:44
  264.2 22.7 %pad_maximum_fusion.1 = bf16[8192,2048]{1,0:T(8,128)(2,1)} fusion(bf16[8192,512]{1,0:T(8,128)(2,1)} %get-tuple-element.278, bf16[8192,512]{1,0:T(8,128)(2,1)} %get-tuple-element.279, bf16[8192,512]{1,0:T(8,128)(2,1)} %get-tuple-element.280, bf16[8192,512]{1,0:T(8,128)(2,1)} %get-tuple-element.277), kind=kLoop, calls=%fused_computation.12 | loop fusion | flops 134217728 | bytes 67108864 | tf_op jit(solution)/shard_map/concatenate | solution.py:61
  287.0 1218.8 %while.19 = (s32[]{:T(128)}, bf16[32,8192]{1,0:T(8,128)(2,1)S(1)}, bf16[4,32,512]{2,1,0:T(8,128)(2,1)S(1)}, f32[4]{0:T(128)S(1)}, pred[]{:T(512)}, /*index=5*/s3...) while((s32[]{:T(128)}, bf16[32,8192]{1,0:T(8,128)(2,1)S(1)}, ...), condition=%wide.region_10.11_spmd.clone, body=%wide.region_4.10_spmd.clone.sunk | while | flops 1343537152 | bytes 52421536 | solution.py:114
  292.4 5.3 all-to-all-start.1
  386.9 4.7 all_to_all.25
  405.2 4.7 all_to_all.25
  423.4 4.7 all_to_all.25
  441.6 4.7 all_to_all.25
  459.9 4.7 all_to_all.25
  478.1 4.7 all_to_all.25
  496.3 4.7 all_to_all.25
  514.6 4.7 all_to_all.25
  532.8 4.7 all_to_all.25
  551.1 4.7 all_to_all.25
  569.3 4.7 all_to_all.25
  587.5 4.7 all_to_all.25
  605.8 4.7 all_to_all.25
  624.0 4.7 all_to_all.25
  642.3 4.7 all_to_all.25
  660.5 4.7 all_to_all.25
  678.7 4.7 all_to_all.25
  697.0 4.7 all_to_all.25
  715.2 4.7 all_to_all.25
  733.5 4.7 all_to_all.25
  751.7 4.7 all_to_all.25
  769.9 4.7 all_to_all.25
  788.2 4.7 all_to_all.25
  806.4 4.7 all_to_all.25
  823.5 490.0 %collective-permute-done = bf16[32,4096]{1,0:T(8,128)(2,1)S(1)} collective-permute-done((bf16[32,4096]{1,0:T(8,128)(2,1)S(1)}, bf16[32,4096]{1,0:T(8,128)(2,1)S(1)}, u32[]{:S(2)}, u32[]{:S(2)}) %collective-permute-start) | collective-permute-done | bytes 262176 | tf_op jit(solution)/shard_map/while/body/eval_jaxpr/ppermute | solution.py:33
  1319.5 19.0 %conditional.3 = (bf16[32,512]{1,0:T(8,128)(2,1)S(1)}, f32[4]{0:T(128)S(1)}, f32[32,512]{1,0:T(8,128)S(1)}) conditional(s32[]{:T(128)} %convert_element_type.178, () %tuple.72, (bf16[32,8192]{1,0:T(8,128)(2,1)S(1)}, bf16[8192,2048]{1,0:T(8,128)(2,1)}, bf16[8192,512]{1,0:T(8,128)(2,1)}) %tuple.73), branch_computations={%region_5.5_spmd, %region_6.8_spmd} | conditional | flops 1342455808 | bytes 44793900 | solution.py:89
  1319.5 4.9 fusion.20
  1324.6 13.6 multiply_reduce_fusion
  1341.4 4.9 all-to-all-start.1
  1357.8 19.0 %conditional.3 = (bf16[32,512]{1,0:T(8,128)(2,1)S(1)}, f32[4]{0:T(128)S(1)}, f32[32,512]{1,0:T(8,128)S(1)}) conditional(s32[]{:T(128)} %convert_element_type.178, () %tuple.72, (bf16[32,8192]{1,0:T(8,128)(2,1)S(1)}, bf16[8192,2048]{1,0:T(8,128)(2,1)}, bf16[8192,512]{1,0:T(8,128)(2,1)}) %tuple.73), branch_computations={%region_5.5_spmd, %region_6.8_spmd} | conditional | flops 1342455808 | bytes 44793900 | solution.py:89
  1357.9 4.9 fusion.20
  1362.9 13.6 multiply_reduce_fusion
  1379.8 4.9 all-to-all-start.1
  1396.2 19.0 %conditional.3 = (bf16[32,512]{1,0:T(8,128)(2,1)S(1)}, f32[4]{0:T(128)S(1)}, f32[32,512]{1,0:T(8,128)S(1)}) conditional(s32[]{:T(128)} %convert_element_type.178, () %tuple.72, (bf16[32,8192]{1,0:T(8,128)(2,1)S(1)}, bf16[8192,2048]{1,0:T(8,128)(2,1)}, bf16[8192,512]{1,0:T(8,128)(2,1)}) %tuple.73), branch_computations={%region_5.5_spmd, %region_6.8_spmd} | conditional | flops 1342455808 | bytes 44793900 | solution.py:89
  1396.2 4.9 fusion.20
  1401.3 13.6 multiply_reduce_fusion
  1418.1 4.9 all-to-all-start.1
  1434.5 19.0 %conditional.3 = (bf16[32,512]{1,0:T(8,128)(2,1)S(1)}, f32[4]{0:T(128)S(1)}, f32[32,512]{1,0:T(8,128)S(1)}) conditional(s32[]{:T(128)} %convert_element_type.178, () %tuple.72, (bf16[32,8192]{1,0:T(8,128)(2,1)S(1)}, bf16[8192,2048]{1,0:T(8,128)(2,1)}, bf16[8192,512]{1,0:T(8,128)(2,1)}) %tuple.73), branch_computations={%region_5.5_spmd, %region_6.8_spmd} | conditional | flops 1342455808 | bytes 44793900 | solution.py:89
  1434.6 4.9 fusion.20
  1439.6 13.6 multiply_reduce_fusion
  1456.5 4.9 all-to-all-start.1
  1472.2 18.7 %collective-permute-start = (bf16[32,4096]{1,0:T(8,128)(2,1)S(1)}, bf16[32,4096]{1,0:T(8,128)(2,1)S(1)}, u32[]{:S(2)}, u32[]{:S(2)}) collective-permute-start(bf16[32,4096]{1,0:T(8,128)(2,1)S(1)} %fusion.27), channel_id=1, source_target_pairs={{0,8},{8,16},{16,24},{24,32},{32,40},{40,48},{48,56},{56,64},{64,7... | collective-permute-start | bytes 786440 | tf_op jit(solution)/shard_map/while/body/eval_jaxpr/ppermute | solution.py:33
  1491.5 5.2 all-to-all-start.1
  (762 shorter events, 491.9 us)
Async XLA Ops:
  288.8 13.3 collective-permute-start
  292.4 9.8 all-to-all-start.1
  308.4 10.7 collective-permute-start
  325.3 10.7 collective-permute-start
  327.8 8.1 all-to-all-start.1
  342.2 10.7 collective-permute-start
  359.1 10.7 collective-permute-start
  361.7 8.1 all-to-all-start.1
  376.1 10.8 collective-permute-start
  393.3 11.8 collective-permute-start
  411.6 11.8 collective-permute-start
  429.8 11.8 collective-permute-start
  448.1 11.8 collective-permute-start
  450.6 8.1 all-to-all-start.1
  466.3 11.8 collective-permute-start
  484.5 11.8 collective-permute-start
  502.8 11.8 collective-permute-start
  505.3 8.1 all-to-all-start.1
  521.0 11.8 collective-permute-start
  539.2 11.8 collective-permute-start
  557.5 11.8 collective-permute-start
  560.0 8.1 all-to-all-start.1
  575.7 11.8 collective-permute-start
  594.0 11.8 collective-permute-start
  612.2 11.8 collective-permute-start
  630.4 11.8 collective-permute-start
  648.7 11.8 collective-permute-start
  651.2 8.1 all-to-all-start.1
  666.9 11.8 collective-permute-start
  685.2 11.8 collective-permute-start
  703.4 11.8 collective-permute-start
  705.9 8.1 all-to-all-start.1
  721.6 11.8 collective-permute-start
  739.9 11.8 collective-permute-start
  758.1 11.8 collective-permute-start
  776.4 11.8 collective-permute-start
  794.6 11.8 collective-permute-start
  812.8 500.7 %collective-permute-start = (bf16[32,4096]{1,0:T(8,128)(2,1)S(1)}, bf16[32,4096]{1,0:T(8,128)(2,1)S(1)}, u32[]{:S(2)}, u32[]{:S(2)}) collective-permute-start(bf16[32,4096]{1,0:T(8,128)(2,1)S(1)} %fusion.27), channel_id=1, source_target_pairs={{0,8},{8,16},{16,24},{24,32},{32,40},{40,48},{48,56},{56,64},{64,7... | collective-permute-start | bytes 786440 | tf_op jit(solution)/shard_map/while/body/eval_jaxpr/ppermute | solution.py:33
  1338.9 13.0 collective-permute-start
  1341.4 9.4 all-to-all-start.1
  1377.3 13.0 collective-permute-start
  1379.8 9.4 all-to-all-start.1
  1415.6 13.0 collective-permute-start
  1418.1 9.4 all-to-all-start.1
  1454.0 12.0 collective-permute-start
  1456.5 9.4 all-to-all-start.1
  1472.2 29.1 %collective-permute-start = (bf16[32,4096]{1,0:T(8,128)(2,1)S(1)}, bf16[32,4096]{1,0:T(8,128)(2,1)S(1)}, u32[]{:S(2)}, u32[]{:S(2)}) collective-permute-start(bf16[32,4096]{1,0:T(8,128)(2,1)S(1)} %fusion.27), channel_id=1, source_target_pairs={{0,8},{8,16},{16,24},{24,32},{32,40},{40,48},{48,56},{56,64},{64,7... | collective-permute-start | bytes 786440 | tf_op jit(solution)/shard_map/while/body/eval_jaxpr/ppermute | solution.py:33
  1491.5 9.7 all-to-all-start.1
  (24 other events, 202.3 us)
